TPU v7x, 32 devices: a whole 2x2x4 slice. The times are simulated.
32 devices in a mesh: grp: 8 (over z, y), rep: 4 (over x, core).
Axes of the slice: x: 2, y: 2, z: 4, core: 2. Of those that a mesh axis runs over, the one named last changes fastest.
Arguments:
- queries: bfloat16 [16, 4, 32, 128], P('grp', 'rep'), may hold values from -3.2 to 3.2
- passages: bfloat16 [512, 4, 180, 128], P('grp', 'rep'), may hold values from -1.796875 to 1.796875
- lengths: int32 [512, 4], P('grp', 'rep'), may hold values from 16 to 180
- cand_ids: int32 [16, 4, 64], P('grp', 'rep'), may hold values from 0 to 511, as said below
- owner_map: int32 [4, 512], P('rep'), may hold values from 0 to 511, as said below
- teacher: float32 [16, 4, 64], P('grp', 'rep'), may hold values from -12 to 312
- weights: float32 [16, 4], P('grp', 'rep'), may hold values from 0.5 to 18
Outputs:
- loss: float32 [], replicated
- query_grad: float32 [16, 4, 32, 128], P('grp', 'rep')
- passage_grad: bfloat16 [512, 4, 180, 128], P('grp', 'rep')
Inputs may be any that keep to these rules, and one draw needn't show every extreme that they name: `cand_ids`: within each replica, the 128 candidates of the queries of one grp index have storage rows of which at most 32 (counted with repeats) lie in any one aligned block of 64 rows; in every draw, in each replica, one block receives exactly 32 from every grp index. `owner_map`: each row is a permutation of 0 to 511.
All inputs are finite; a program needn't handle non-finite values.
Results may differ from a plain program's by a relative error of at most 0.0055.
Values may be sent and summed in bfloat16 or wider, within the bound.
A program may use at most 128 MiB of HBM per device.

v0:
```python
import functools
import math

import jax
import jax.numpy as jnp
from jax import lax
from jax.experimental import pallas as pl
from jax.experimental.pallas import tpu as pltpu
from jax.sharding import PartitionSpec as P

temper = 0.05
to_base2 = 1.0 / (temper * math.log(2.0))
LANES = 128
MESH = pl.DeviceIdType.MESH
HIGH = lax.Precision.HIGHEST
VMEM_SPEC = pl.BlockSpec(memory_space=pltpu.VMEM)


def greet(groups, replicas, me, mine):
    barrier = pltpu.get_barrier_semaphore()
    for step in range(1, groups):
        pl.semaphore_signal(
            barrier, inc=1, device_id={"grp": lax.rem(me + step, groups)}, device_id_type=MESH
        )
    for step in range(1, replicas):
        pl.semaphore_signal(
            barrier, inc=1, device_id={"rep": lax.rem(mine + step, replicas)}, device_id_type=MESH
        )


def greeted(groups, replicas):
    pl.semaphore_wait(pltpu.get_barrier_semaphore(), groups - 1 + replicas - 1)


def share_kernel(
    groups, block, queries_ref, cand_ref, map_ref, teacher_ref, weights_ref,
    all_queries, all_meta, query_buf, meta_buf, send_sem, recv_sem,
):
    me = lax.axis_index("grp")
    greet(groups, 1, me, 0)
    count, ways = cand_ref.shape
    table = map_ref[...].astype(jnp.float32)
    ids = lax.broadcasted_iota(jnp.int32, (ways, table.shape[1]), 1)
    diagonal = lax.broadcasted_iota(jnp.int32, (ways, ways), 0) == lax.broadcasted_iota(
        jnp.int32, (ways, ways), 1
    )
    teacher = teacher_ref[...]
    top = jnp.max(teacher, axis=1, keepdims=True)
    log_teacher = teacher - top
    log_teacher = log_teacher - jnp.log(jnp.sum(jnp.exp(log_teacher), axis=1, keepdims=True))
    prob = jnp.exp(log_teacher)
    entropy = jnp.sum(prob * log_teacher, axis=1, keepdims=True)
    meta_buf[me] = jnp.zeros(meta_buf.shape[1:], jnp.float32)
    for q in range(count):
        line = cand_ref[q : q + 1, :].astype(jnp.float32)
        column = jnp.sum(jnp.where(diagonal, line, 0.0), axis=1, keepdims=True).astype(jnp.int32)
        row = jnp.sum(jnp.where(column == ids, table, 0.0), axis=1, keepdims=True)
        row = jnp.sum(jnp.where(diagonal, row, 0.0), axis=0, keepdims=True)
        meta_buf[me, q : q + 1, :ways] = row
    meta_buf[me, count : 2 * count, :ways] = prob
    for q in range(count):
        meta_buf[me, 2 * count + q : 2 * count + q + 1, :] = jnp.broadcast_to(
            weights_ref[:, q : q + 1], (1, LANES)
        )
    meta_buf[me, 3 * count : 4 * count, :] = jnp.broadcast_to(entropy, (count, LANES))
    query_buf[me] = queries_ref[...]
    greeted(groups, 1)
    copies = []
    for step in range(1, groups):
        peer = lax.rem(me + step, groups)
        for which, buf in enumerate((query_buf, meta_buf)):
            copies.append(
                pltpu.make_async_remote_copy(
                    src_ref=buf.at[me],
                    dst_ref=buf.at[me],
                    send_sem=send_sem.at[which, step],
                    recv_sem=recv_sem.at[which, step],
                    device_id={"grp": peer},
                    device_id_type=MESH,
                )
            )
            copies[-1].start()
    for copy in copies:
        copy.wait()
    all_queries[...] = query_buf[...]
    all_meta[...] = meta_buf[...]


def span_of(tokens, limit):
    return max(size for size in range(1, limit + 1) if tokens % size == 0)


def lengths_of(lengths_ref, first, rows, width):
    index = lax.broadcasted_iota(jnp.int32, (rows, width), 0)
    found = jnp.zeros((rows, width), jnp.int32)
    for k in range(rows):
        found = jnp.where(index == k, lengths_ref[first + k], found)
    return found


def forward_kernel(
    count, ways, block, lengths_ref, passages_ref, queries_ref, meta_ref,
    lse_ref, score_ref, hits_ref, mass_ref, held, all_lse,
):
    step = pl.program_id(0)
    part = pl.program_id(1)
    groups = meta_ref.shape[0]
    tokens, rows, dim = passages_ref.shape
    width = queries_ref.shape[0]
    slot = score_ref.shape[1]

    @pl.when((step == 0) & (part == 0))
    def _():
        spots = lax.broadcasted_iota(jnp.int32, (ways, groups * slot), 1)
        for source in range(groups):
            turned = jnp.transpose(meta_ref[source])
            for q in range(count):
                row = turned[:ways, q : q + 1].astype(jnp.int32)
                spot = row + (slot - block) * (row // block)
                hot = spot == spots
                place = source * count + q
                hits_ref[place : place + 1, :] = jnp.sum(
                    jnp.where(hot, 1.0, 0.0), axis=0, keepdims=True
                )
                mass_ref[place : place + 1, :] = jnp.sum(
                    jnp.where(hot, turned[:ways, count + q : count + q + 1], 0.0),
                    axis=0,
                    keepdims=True,
                )

    lengths = lengths_of(lengths_ref, step * rows, rows, width)
    size = span_of(tokens, 20)
    highest = jnp.full((rows, width), -1e30, jnp.float32)
    for first in range(0, tokens, size):
        products = lax.dot_general(
            passages_ref[first : first + size].reshape(size * rows, dim), queries_ref[...],
            (((1,), (1,)), ((), ())), preferred_element_type=jnp.float32,
        )
        for j in range(size):
            scaled = jnp.where(
                first + j < lengths, products[j * rows : (j + 1) * rows] * to_base2, -1e30
            )
            held[first + j] = scaled
            highest = jnp.maximum(highest, scaled)
    summed = jnp.zeros((rows, width), jnp.float32)
    for j in range(tokens):
        summed = summed + jnp.exp2(held[j] - highest)
    lse = highest + jnp.log2(summed)
    lse_ref[...] = lse
    all_lse[step, part] = lse

    @pl.when((step == pl.num_programs(0) - 1) & (part == pl.num_programs(1) - 1))
    def _():
        total = score_ref.shape[0]
        parts = all_lse.shape[1]
        each = width * parts // total
        score_ref[...] = jnp.zeros_like(score_ref)
        belongs = lax.broadcasted_iota(jnp.int32, (total // parts, width), 1) // each
        pick = jnp.where(
            belongs == lax.broadcasted_iota(jnp.int32, (total // parts, width), 0), 1.0, 0.0
        )
        span = total // parts
        for k in range(parts):
            matched = jnp.concatenate(
                [all_lse[i, k] for i in range(all_lse.shape[0])], axis=0
            ) * (1.0 / to_base2)
            score_ref[k * span : (k + 1) * span, :block] = lax.dot_general(
                pick, matched, (((1,), (1,)), ((), ())),
                precision=HIGH, preferred_element_type=jnp.float32,
            )


def grade_kernel(
    groups, replicas, score_ref, hits_ref, mass_ref, meta_ref, grad_ref, loss_ref,
    score_buf, weight_buf, grad_buf, query_weight, query_entropy,
    send_sem, recv_sem, wsend_sem, wrecv_sem,
):
    me = lax.axis_index("grp")
    mine = lax.axis_index("rep")
    greet(groups, replicas, me, mine)
    total, slot = score_ref.shape
    count = total // groups
    for source in range(groups):
        span = slice(source * count, (source + 1) * count)
        query_weight[span, :] = meta_ref[source, 2 * count : 3 * count, :]
        query_entropy[span, :] = meta_ref[source, 3 * count : 4 * count, :]
    weights = query_weight[:, :1]
    score_buf[me] = score_ref[...]
    weight_buf[mine] = jnp.broadcast_to(
        jnp.sum(query_weight[...], axis=0, keepdims=True), weight_buf.shape[1:]
    )
    greeted(groups, replicas)
    copies = []
    for step in range(1, groups):
        copies.append(
            pltpu.make_async_remote_copy(
                src_ref=score_buf.at[me],
                dst_ref=score_buf.at[me],
                send_sem=send_sem.at[step],
                recv_sem=recv_sem.at[step],
                device_id={"grp": lax.rem(me + step, groups)},
                device_id_type=MESH,
            )
        )
        copies[-1].start()
    for step in range(1, replicas):
        copies.append(
            pltpu.make_async_remote_copy(
                src_ref=weight_buf.at[mine],
                dst_ref=weight_buf.at[mine],
                send_sem=wsend_sem.at[step],
                recv_sem=wrecv_sem.at[step],
                device_id={"rep": lax.rem(mine + step, replicas)},
                device_id_type=MESH,
            )
        )
        copies[-1].start()
    for copy in copies:
        copy.wait()
    weight_sum = jnp.sum(weight_buf[...], axis=0)[:1, :1]
    scores = jnp.concatenate([score_buf[owner] for owner in range(groups)], axis=1)
    hits = hits_ref[...]
    mass = mass_ref[...]
    asked = hits > 0.0
    held = jnp.where(asked, scores, -1e30)
    highest = jnp.max(held, axis=1, keepdims=True)
    summed = jnp.sum(hits * jnp.exp(held - highest), axis=1, keepdims=True)
    log_student = jnp.where(asked, scores - (highest + jnp.log(summed)), -1e30)
    student = hits * jnp.exp(log_student)
    crossed = jnp.sum(jnp.where(asked, mass * log_student, 0.0), axis=1, keepdims=True)
    divergence = query_entropy[:, :1] - crossed
    grad_buf[...] = (total * replicas) * weights / weight_sum * (student - mass)
    own = grad_buf[:, pl.ds(pl.multiple_of(me * slot, slot), slot)]
    width = grad_ref.shape[1]
    each = width // total
    belongs = lax.broadcasted_iota(jnp.int32, (total, width), 1) // each
    pick = jnp.where(belongs == lax.broadcasted_iota(jnp.int32, (total, width), 0), 1.0, 0.0)
    spread = lax.dot_general(
        own, pick, (((0,), (0,)), ((), ())), precision=HIGH, preferred_element_type=jnp.float32
    )
    grad_ref[...] = spread[: grad_ref.shape[0]]
    loss_ref[...] = jnp.broadcast_to(
        jnp.sum(weights * divergence, axis=0, keepdims=True) / weight_sum, loss_ref.shape
    )


def backward_kernel(
    lengths_ref, passages_ref, queries_ref, lse_ref, grad_ref, out_ref, partial_ref,
    total, token_total,
):
    step = pl.program_id(0)
    part = pl.program_id(1)
    parts = total.shape[0]
    tokens, rows, dim = passages_ref.shape
    width = queries_ref.shape[0]

    @pl.when(step == 0)
    def _():
        total[part] = jnp.zeros(total.shape[1:], jnp.float32)

    if parts > 1:

        @pl.when(part == 0)
        def _():
            token_total[...] = jnp.zeros_like(token_total)

    lengths = lengths_of(lengths_ref, step * rows, rows, width)[None]
    lse = lse_ref[...][None]
    grad = grad_ref[...][None]
    queries = queries_ref[...]
    size = span_of(tokens, 36)
    added = None
    for first in range(0, tokens, size):
        passage = passages_ref[first : first + size].reshape(size * rows, dim)
        products = lax.dot_general(
            passage, queries, (((1,), (1,)), ((), ())), preferred_element_type=jnp.float32
        ).reshape(size, rows, width)
        position = first + lax.broadcasted_iota(jnp.int32, (size, 1, 1), 0)
        powers = jnp.exp2(jnp.where(position < lengths, products * to_base2 - lse, -1e30))
        scaled_grad = (powers * grad).astype(jnp.bfloat16).reshape(size * rows, width)
        token_grad = jnp.dot(scaled_grad, queries, preferred_element_type=jnp.float32).reshape(
            size, rows, dim
        )
        if parts > 1:
            token_total[first : first + size] += token_grad
        else:
            out_ref[first : first + size] = token_grad.astype(jnp.bfloat16)
        piece = lax.dot_general(
            passage, scaled_grad, (((0,), (0,)), ((), ())), preferred_element_type=jnp.float32
        )
        added = piece if added is None else added + piece
    total[part] += added

    if parts > 1:

        @pl.when(part == parts - 1)
        def _():
            out_ref[...] = token_total[...].astype(jnp.bfloat16)

    @pl.when(step == pl.num_programs(0) - 1)
    def _():
        partial_ref[pl.ds(pl.multiple_of(part * width, width), width), :] = jnp.transpose(
            total[part]
        ).astype(partial_ref.dtype)


def collect_kernel(
    groups, replicas, partial_ref, loss_ref, grad_ref, loss_out,
    arrived, loss_buf, send_sem, recv_sem, lsend_sem, lrecv_sem,
):
    me = lax.axis_index("grp")
    mine = lax.axis_index("rep")
    greet(groups, replicas, me, mine)
    loss_buf[mine] = loss_ref[...]
    greeted(groups, replicas)
    copies = []
    for step in range(1, groups):
        peer = lax.rem(me + step, groups)
        copies.append(
            pltpu.make_async_remote_copy(
                src_ref=partial_ref.at[peer],
                dst_ref=arrived.at[me],
                send_sem=send_sem.at[step],
                recv_sem=recv_sem.at[step],
                device_id={"grp": peer},
                device_id_type=MESH,
            )
        )
        copies[-1].start()
    for step in range(1, replicas):
        copies.append(
            pltpu.make_async_remote_copy(
                src_ref=loss_buf.at[mine],
                dst_ref=loss_buf.at[mine],
                send_sem=lsend_sem.at[step],
                recv_sem=lrecv_sem.at[step],
                device_id={"rep": lax.rem(mine + step, replicas)},
                device_id_type=MESH,
            )
        )
        copies[-1].start()
    arrived[me] = partial_ref[me]
    for copy in copies:
        copy.wait()
    grad_ref[...] = jnp.sum(arrived[...].astype(jnp.float32), axis=0)
    loss_out[...] = jnp.sum(loss_buf[...], axis=0)[:1, :1]


def on_device(queries, passages, lengths, cand_ids, owner_map, teacher, weights):
    groups = lax.axis_size("grp")
    replicas = lax.axis_size("rep")
    count, _, query_len, dim = queries.shape
    block, _, tokens, _ = passages.shape
    ways = cand_ids.shape[2]
    own_rows = count * query_len
    width = groups * own_rows
    total = groups * count
    slot = -(-block // LANES) * LANES
    f32 = jnp.float32
    dma = pltpu.SemaphoreType.DMA
    meta_rows = -(-4 * count // 8) * 8
    all_queries, all_meta = pl.pallas_call(
        functools.partial(share_kernel, groups, block),
        name="share",
        out_shape=[
            jax.ShapeDtypeStruct((groups, own_rows, dim), queries.dtype),
            jax.ShapeDtypeStruct((groups, meta_rows, LANES), f32),
        ],
        in_specs=[VMEM_SPEC] * 5,
        out_specs=[VMEM_SPEC] * 2,
        scratch_shapes=[
            pltpu.VMEM((groups, own_rows, dim), queries.dtype),
            pltpu.VMEM((groups, meta_rows, LANES), f32),
            dma((2, groups)),
            dma((2, groups)),
        ],
        compiler_params=pltpu.CompilerParams(collective_id=0, has_side_effects=True),
    )(
        queries.reshape(own_rows, dim),
        cand_ids[:, 0],
        owner_map,
        teacher[:, 0],
        jnp.transpose(weights),
    )
    flat_queries = all_queries.reshape(width, dim)
    flat_passages = jnp.transpose(passages[:, 0], (1, 0, 2))
    flat_lengths = lengths.reshape(block)
    rows = 16 if block % 16 == 0 else block
    chunk = width if width <= 512 else width // (width // 512)
    parts = width // chunk
    grid = (block // rows, parts)
    whole = lambda *shape: pl.BlockSpec(shape, lambda i, k, *_: (0,) * len(shape))
    passage_spec = pl.BlockSpec((tokens, rows, dim), lambda i, k, *_: (0, i, 0))
    query_spec = pl.BlockSpec((chunk, dim), lambda i, k, *_: (k, 0))
    row_spec = pl.BlockSpec((rows, chunk), lambda i, k, *_: (i, k))
    both = pltpu.CompilerParams(dimension_semantics=("arbitrary", "arbitrary"))
    lse, score, hits, mass = pl.pallas_call(
        functools.partial(forward_kernel, count, ways, block),
        name="forward",
        grid_spec=pltpu.PrefetchScalarGridSpec(
            num_scalar_prefetch=1,
            grid=grid,
            in_specs=[passage_spec, query_spec, whole(groups, meta_rows, LANES)],
            out_specs=[
                row_spec,
                whole(total, slot),
                whole(total, groups * slot),
                whole(total, groups * slot),
            ],
            scratch_shapes=[
                pltpu.VMEM((tokens, rows, chunk), f32),
                pltpu.VMEM((*grid, rows, chunk), f32),
            ],
        ),
        out_shape=[
            jax.ShapeDtypeStruct((block, width), f32),
            jax.ShapeDtypeStruct((total, slot), f32),
            jax.ShapeDtypeStruct((total, groups * slot), f32),
            jax.ShapeDtypeStruct((total, groups * slot), f32),
        ],
        compiler_params=both,
    )(flat_lengths, flat_passages, flat_queries, all_meta)
    grad, loss_part = pl.pallas_call(
        functools.partial(grade_kernel, groups, replicas),
        name="grade",
        out_shape=[
            jax.ShapeDtypeStruct((block, width), f32),
            jax.ShapeDtypeStruct((8, LANES), f32),
        ],
        in_specs=[VMEM_SPEC] * 4,
        out_specs=[VMEM_SPEC] * 2,
        scratch_shapes=[
            pltpu.VMEM((groups, total, slot), f32),
            pltpu.VMEM((replicas, 8, LANES), f32),
            pltpu.VMEM((total, groups * slot), f32),
            pltpu.VMEM((total, LANES), f32),
            pltpu.VMEM((total, LANES), f32),
            dma((groups,)),
            dma((groups,)),
            dma((replicas,)),
            dma((replicas,)),
        ],
        compiler_params=pltpu.CompilerParams(collective_id=1, has_side_effects=True),
    )(score, hits, mass, all_meta)
    passage_grad, partial = pl.pallas_call(
        backward_kernel,
        name="backward",
        grid_spec=pltpu.PrefetchScalarGridSpec(
            num_scalar_prefetch=1,
            grid=grid,
            in_specs=[passage_spec, query_spec, row_spec, row_spec],
            out_specs=[passage_spec, whole(width, dim)],
            scratch_shapes=[
                pltpu.VMEM((parts, dim, chunk), f32),
                pltpu.VMEM((tokens, rows, dim) if parts > 1 else (8, rows, dim), f32),
            ],
        ),
        out_shape=[
            jax.ShapeDtypeStruct((tokens, block, dim), jnp.bfloat16),
            jax.ShapeDtypeStruct((width, dim), jnp.bfloat16),
        ],
        compiler_params=both,
    )(flat_lengths, flat_passages, flat_queries, lse, grad)
    query_grad, loss = pl.pallas_call(
        functools.partial(collect_kernel, groups, replicas),
        name="collect",
        out_shape=[
            jax.ShapeDtypeStruct((own_rows, dim), f32),
            jax.ShapeDtypeStruct((1, 1), f32),
        ],
        in_specs=[VMEM_SPEC] * 2,
        out_specs=[VMEM_SPEC] * 2,
        scratch_shapes=[
            pltpu.VMEM((groups, own_rows, dim), jnp.bfloat16),
            pltpu.VMEM((replicas, 8, LANES), f32),
            dma((groups,)),
            dma((groups,)),
            dma((replicas,)),
            dma((replicas,)),
        ],
        compiler_params=pltpu.CompilerParams(collective_id=2, has_side_effects=True),
    )(partial.reshape(groups, own_rows, dim), loss_part)
    return (
        loss.reshape(()),
        query_grad.reshape(count, 1, query_len, dim),
        jnp.transpose(passage_grad, (1, 0, 2))[:, None],
    )


def solution(mesh):
    return jax.shard_map(
        on_device,
        mesh=mesh,
        in_specs=(
            P("grp", "rep", None, None),
            P("grp", "rep", None, None),
            P("grp", "rep"),
            P("grp", "rep", None),
            P("rep", None),
            P("grp", "rep", None),
            P("grp", "rep"),
        ),
        out_specs=(P(), P("grp", "rep", None, None), P("grp", "rep", None, None)),
        check_vma=False,
    )
```

profile of v0, /device:TPU:0, one launch (start us, length us, event | category | flops | bytes accessed | tf_op | source)
XLA Modules:
  0.0 60.1 jit_solution(2324693448389282421)
XLA Ops:
  0.6 11.2 %share.1 = (bf16[8,64,128]{2,1,0:T(8,128)(2,1)}, f32[8,8,128]{2,1,0:T(8,128)}) custom-call(bf16[64,128]{1,0:T(8,128)(2,1)} %bitcast.23, s32[2,64]{1,0:T(2,128)} %bitcast.26, s32[1,512]{1,0:T(1,128)} %map_ref.1, f32[2,64]{1,0:T(2,128)} %bitcast.27, f32[1,2]{1,0:T(1,128)} %bitcast.28), custom_call_target="tpu_custom_call" | custom-call | tf_op jit(solution)/shard_map/share/pallas_call | solution.py:362
  11.8 12.0 %forward.1 = (f32[64,512]{1,0:T(8,128)}, f32[16,128]{1,0:T(8,128)}, f32[16,1024]{1,0:T(8,128)}, f32[16,1024]{1,0:T(8,128)}) custom-call(s32[64]{0:T(128)} %bitcast.24, bf16[180,64,128]{2,1,0:T(8,128)(2,1)} %bitcast.17, bf16[512,128]{1,0:T(8,128)(2,1)} %bitcast.19, f32[8,8,128]{2,1,0:T(8,128)} %get-tuple-element.16.meta_ref), custom_call_target="tpu_custom_call" | custom-call | tf_op jit(solution)/shard_map/forward/pallas_call | solution.py:397
  23.8 10.1 %grade.1 = (f32[64,512]{1,0:T(8,128)}, f32[8,128]{1,0:T(8,128)}) custom-call(f32[16,128]{1,0:T(8,128)} %get-tuple-element.18.score_ref, f32[16,1024]{1,0:T(8,128)} %get-tuple-element.19.hits_ref, f32[16,1024]{1,0:T(8,128)} %get-tuple-element.20.mass_ref, f32[8,8,128]{2,1,0:T(8,128)} %get-tuple-element.16.meta_ref), custom_call_target="tpu_custom_call" | custom-call | tf_op jit(solution)/shard_map/grade/pallas_call | solution.py:423
  33.9 14.1 %backward.1 = (bf16[180,64,128]{2,1,0:T(8,128)(2,1)}, bf16[512,128]{1,0:T(8,128)(2,1)}) custom-call(s32[64]{0:T(128)} %bitcast.25, bf16[180,64,128]{2,1,0:T(8,128)(2,1)} %bitcast.18, bf16[512,128]{1,0:T(8,128)(2,1)} %bitcast.20, f32[64,512]{1,0:T(8,128)} %get-tuple-element.17.lse_ref, f32[64,512]{1,0:T(8,128)} %get-tuple-element.21.grad_ref), custom_call_target="tpu_custom_call" | custom-call | tf_op jit(solution)/shard_map/backward/pallas_call | solution.py:445
  48.1 8.9 %collect.1 = (f32[64,128]{1,0:T(8,128)}, f32[1,1]{1,0:T(1,128)}) custom-call(bf16[8,64,128]{2,1,0:T(8,128)(2,1)} %bitcast.21, f32[8,128]{1,0:T(8,128)} %get-tuple-element.23.loss_ref), custom_call_target="tpu_custom_call" | custom-call | tf_op jit(solution)/shard_map/collect/pallas_call | solution.py:464
  57.6 1.4 %copy.14 = f32[2,1,32,128]{3,2,1,0:T(8,128)} copy(f32[2,1,32,128]{3,2,1,0:T(8,128)} %bitcast.22) | data formatting | bytes 65536
where the time goes:
time: 60.5 us; the launch traced here: 60.1 us
  Pallas kernels  56.3 us (93%)
  between operations  2.47 us (4%)
  local copies, waits for them, and re-layouts  1.38 us (2%)
    pallas_call x1, Pallas kernels, on_device(): pl.pallas_call(backward_kernel, name='backward', grid_spec=pltpu.Prefetch...  14.1 us
    pallas_call x1, Pallas kernels, on_device(): pl.pallas_call(functools.partial(forward_kernel, count, ways, block), nam...  12 us
    pallas_call x1, Pallas kernels, on_device(): pl.pallas_call(functools.partial(share_kernel, groups, block), name='shar...  11.2 us
    pallas_call x1, Pallas kernels, on_device(): pl.pallas_call(functools.partial(grade_kernel, groups, replicas), name='g...  10.1 us
    pallas_call x1, Pallas kernels, on_device(): pl.pallas_call(functools.partial(collect_kernel, groups, replicas), name=...  8.87 us
    unnamed x1, local copies, waits for them, and re-layouts  1.38 us

commit v1 on v0

--- a/solution.py
+++ b/solution.py
@@ -487,9 +487,459 @@
     )
 
 
+def partner(me, turn):
+    peer = me
+    bit = 1
+    while bit <= turn:
+        if turn & bit:
+            peer = peer + bit * (1 - 2 * lax.rem(lax.div(me, bit), 2))
+        bit *= 2
+    return peer
+
+
+def share_meta(me, cand, table, teacher, weights, meta_buf):
+    count, ways = cand.shape
+    ids = lax.broadcasted_iota(jnp.int32, (ways, table.shape[1]), 1)
+    diagonal = lax.broadcasted_iota(jnp.int32, (ways, ways), 0) == lax.broadcasted_iota(
+        jnp.int32, (ways, ways), 1
+    )
+    top = jnp.max(teacher, axis=1, keepdims=True)
+    log_teacher = teacher - top
+    log_teacher = log_teacher - jnp.log(jnp.sum(jnp.exp(log_teacher), axis=1, keepdims=True))
+    prob = jnp.exp(log_teacher)
+    entropy = jnp.sum(prob * log_teacher, axis=1, keepdims=True)
+    meta_buf[me] = jnp.zeros(meta_buf.shape[1:], jnp.float32)
+    for q in range(count):
+        line = cand[q : q + 1, :].astype(jnp.float32)
+        column = jnp.sum(jnp.where(diagonal, line, 0.0), axis=1, keepdims=True).astype(jnp.int32)
+        row = jnp.sum(jnp.where(column == ids, table, 0.0), axis=1, keepdims=True)
+        row = jnp.sum(jnp.where(diagonal, row, 0.0), axis=0, keepdims=True)
+        meta_buf[me, q : q + 1, :ways] = row
+    meta_buf[me, count : 2 * count, :ways] = prob
+    for q in range(count):
+        meta_buf[me, 2 * count + q : 2 * count + q + 1, :] = jnp.broadcast_to(
+            weights[:, q : q + 1], (1, LANES)
+        )
+    meta_buf[me, 3 * count : 4 * count, :] = jnp.broadcast_to(entropy, (count, LANES))
+
+
+def place_candidates(count, ways, meta_ref, hits_ref, mass_ref):
+    groups = meta_ref.shape[0]
+    spots = lax.broadcasted_iota(jnp.int32, (ways, hits_ref.shape[1]), 1)
+    for source in range(groups):
+        turned = jnp.transpose(meta_ref[source])
+        for q in range(count):
+            hot = turned[:ways, q : q + 1].astype(jnp.int32) == spots
+            place = source * count + q
+            hits_ref[place : place + 1, :] = jnp.sum(
+                jnp.where(hot, 1.0, 0.0), axis=0, keepdims=True
+            )
+            mass_ref[place : place + 1, :] = jnp.sum(
+                jnp.where(hot, turned[:ways, count + q : count + q + 1], 0.0),
+                axis=0,
+                keepdims=True,
+            )
+
+
+def fused_kernel(
+    groups, replicas,
+    queries_hbm, cand_hbm, map_hbm, teacher_hbm, weights_hbm, lengths_hbm, passages_hbm,
+    out_ref, grad_ref, loss_ref,
+    raw, doubled, cleared, held, power, inverse, lse, query_buf, folded, meta_buf,
+    hits_ref, mass_ref, pick_ref, score_buf, weight_buf, grade_buf, query_weight, query_entropy,
+    partial_buf, arrived, loss_buf, cand_ref, map_ref, teacher_ref, weights_ref, lengths_ref,
+    load_sem, small_sem, send_sem, recv_sem, wsend_sem, wrecv_sem,
+):
+    f32, bf16 = jnp.float32, jnp.bfloat16
+    me = lax.axis_index("grp")
+    mine = lax.axis_index("rep")
+    greet(groups, replicas, me, mine)
+    tokens, block, dim = raw.shape
+    count, ways = cand_ref.shape
+    own_rows = query_buf.shape[1]
+    width = groups * own_rows
+    half = width // 2
+    total = groups * count
+    rows = held.shape[2]
+    blocks = block // rows
+    own_copy = pltpu.make_async_copy(queries_hbm, query_buf.at[0], small_sem.at[0])
+    own_copy.start()
+    loads = []
+    pieces = load_sem.shape[0]
+    for k in range(pieces):
+        at = pl.ds(k * (tokens // pieces), tokens // pieces)
+        loads.append(pltpu.make_async_copy(passages_hbm.at[at], raw.at[at], load_sem.at[k]))
+    small = []
+    for k, (there, here) in enumerate(
+        (
+            (cand_hbm, cand_ref), (map_hbm, map_ref), (teacher_hbm, teacher_ref),
+            (weights_hbm, weights_ref), (lengths_hbm, lengths_ref),
+        )
+    ):
+        small.append(pltpu.make_async_copy(there, here, small_sem.at[1 + k]))
+    for copy in small + loads:
+        copy.start()
+
+    def exchange(source, target, which, turns):
+        copies = {}
+        for turn in turns:
+            copies[turn] = pltpu.make_async_remote_copy(
+                src_ref=source(turn),
+                dst_ref=target(turn),
+                send_sem=send_sem.at[which, turn],
+                recv_sem=recv_sem.at[which, turn],
+                device_id={"grp": partner(me, turn)},
+                device_id_type=MESH,
+            )
+            copies[turn].start()
+        return copies
+
+    def across(buf, which):
+        copies = []
+        for step in range(1, replicas):
+            copies.append(
+                pltpu.make_async_remote_copy(
+                    src_ref=buf.at[mine],
+                    dst_ref=buf.at[mine],
+                    send_sem=wsend_sem.at[which, step],
+                    recv_sem=wrecv_sem.at[which, step],
+                    device_id={"rep": lax.rem(mine + step, replicas)},
+                    device_id_type=MESH,
+                )
+            )
+            copies[-1].start()
+        return copies
+
+    near = range(1, groups)
+    far = range(groups - 1, 0, -1)
+    own_copy.wait()
+    greeted(groups, replicas)
+    query_copies = exchange(lambda _: query_buf.at[0], lambda t: query_buf.at[t], 0, near)
+
+    for copy in small:
+        copy.wait()
+    share_meta(
+        me, cand_ref[...], map_ref[...].astype(f32), teacher_ref[...], weights_ref[...], meta_buf
+    )
+    meta_copies = exchange(lambda _: meta_buf.at[me], lambda _: meta_buf.at[me], 1, far)
+
+    wide = jnp.transpose(
+        jnp.broadcast_to(lengths_ref[...].astype(f32), (LANES, lengths_ref.shape[1]))
+    )
+    wide16 = wide.astype(bf16)
+    column = lax.broadcasted_iota(jnp.int32, (1, width), 1)
+    each = own_rows // count
+    turn = column // own_rows
+    source = jnp.zeros_like(turn)
+    for k in range(groups):
+        source = jnp.where(turn == k, partner(me, k), source)
+    query = source * count + (column - turn * own_rows) // each
+    pick = jnp.where(query == lax.broadcasted_iota(jnp.int32, (total, width), 0), 1.0, 0.0)
+    pick_ref[...] = pick
+    for copy in loads:
+        copy.wait()
+    first_token = raw[0]
+    prep = span_of(tokens, 12)
+
+    def prepare(k, _):
+        for j in range(prep):
+            at = k * prep + j
+            here = raw[at]
+            usable = at.astype(f32).astype(bf16) < wide16
+            known = jnp.where(usable, here, first_token)
+            doubled[at, :, :dim] = known
+            doubled[at, :, dim:] = known
+            cleared[at] = jnp.where(usable, here, jnp.zeros_like(here))
+        return 0
+
+    lax.fori_loop(0, tokens // prep, prepare, 0)
+
+    bite = span_of(tokens, 4)
+    units = [(h, b) for h in range(2) for b in range(blocks)]
+    above = None
+    for u in range(len(units) + 1):
+        if u < len(units):
+            h, b = units[u]
+            if b == 0:
+                span = slice(h * (groups // 2), (h + 1) * (groups // 2))
+                for t in range(groups)[span]:
+                    if t:
+                        query_copies[t].wait()
+                scaled = query_buf[span].reshape(half, dim).astype(f32) * to_base2
+                upper = scaled.astype(bf16)
+                folded[h, :, :dim] = upper
+                folded[h, :, dim:] = (scaled - upper.astype(f32)).astype(bf16)
+            products = lax.dot_general(
+                doubled[:, b * rows : (b + 1) * rows, :].reshape(tokens * rows, 2 * dim),
+                folded[h], (((1,), (1,)), ((), ())), preferred_element_type=f32,
+            ).reshape(tokens, rows, half)
+            highest = None
+        if u > 0:
+            h0, b0 = units[u - 1]
+            summed = jnp.zeros((rows, half), f32)
+        for first in range(0, tokens, bite):
+            at = slice(first, first + bite)
+            if u < len(units):
+                held[u % 2, at] = products[at]
+                top = jnp.max(products[at], axis=0)
+                highest = top if highest is None else jnp.maximum(highest, top)
+            if u > 0:
+                powers = jnp.exp2(held[(u - 1) % 2, at] - above[None])
+                power[h0, b0, at] = powers.astype(bf16)
+                summed = summed + jnp.sum(powers, axis=0)
+        if u > 0:
+            at = slice(b0 * rows, (b0 + 1) * rows)
+            to = slice(h0 * half, (h0 + 1) * half)
+            unused = (tokens - wide[at, :1]) * jnp.exp2(held[(u - 1) % 2, 0] - above)
+            summed = summed - unused
+            lse[at, to] = above + jnp.log2(summed)
+            inverse[at, to] = 1.0 / summed
+        above = highest
+
+    scores = lax.dot_general(
+        pick_ref[...], lse[...] * (1.0 / to_base2), (((1,), (1,)), ((), ())),
+        precision=HIGH, preferred_element_type=f32,
+    )
+    score_buf[me, :, :block] = scores[: total // 2]
+    score_buf[me, :, block:] = scores[total // 2 :]
+    score_copies = exchange(lambda _: score_buf.at[me], lambda _: score_buf.at[me], 2, far)
+    for t in meta_copies:
+        meta_copies[t].wait()
+    for owner in range(groups):
+        at = slice(owner * count, (owner + 1) * count)
+        query_weight[at, :] = meta_buf[owner, 2 * count : 3 * count, :]
+        query_entropy[at, :] = meta_buf[owner, 3 * count : 4 * count, :]
+    weight_buf[mine] = jnp.broadcast_to(
+        jnp.sum(query_weight[...], axis=0, keepdims=True), weight_buf.shape[1:]
+    )
+    weight_copies = across(weight_buf, 0)
+    place_candidates(count, ways, meta_buf, hits_ref, mass_ref)
+    for copy in weight_copies:
+        copy.wait()
+    weights = query_weight[:, :1]
+    weight_sum = jnp.sum(weight_buf[...], axis=0)[:1, :1]
+    factor = (total * replicas) * weights / weight_sum
+    hits = hits_ref[...]
+    mass = mass_ref[...]
+    asked = hits > 0.0
+    for t in score_copies:
+        score_copies[t].wait()
+    left = lax.broadcasted_iota(jnp.int32, (total // 2, LANES), 1) < block
+    tiles = []
+    for owner in range(0, groups, 2):
+        one, two = score_buf[owner], score_buf[owner + 1]
+        tiles.append(
+            jnp.concatenate(
+                [
+                    jnp.where(left, one, pltpu.roll(two, block, 1)),
+                    jnp.where(left, pltpu.roll(one, block, 1), two),
+                ],
+                axis=0,
+            )
+        )
+    scores = jnp.concatenate(tiles, axis=1)
+    masked = jnp.where(asked, scores, -1e30)
+    highest = jnp.max(masked, axis=1, keepdims=True)
+    summed = jnp.sum(hits * jnp.exp(masked - highest), axis=1, keepdims=True)
+    log_student = jnp.where(asked, scores - (highest + jnp.log(summed)), -1e30)
+    grade_buf[...] = factor * (hits * jnp.exp(log_student) - mass)
+    pair = grade_buf[:, pl.ds(pl.multiple_of(lax.div(me, 2) * LANES, LANES), LANES)]
+    odd = jnp.broadcast_to(lax.rem(me, 2), pair.shape) == 1
+    own = jnp.where(odd, pltpu.roll(pair, block, 1), pair)[:, :block]
+    upper = own.astype(bf16)
+    lower = (own - upper.astype(f32)).astype(bf16)
+    pick16 = pick_ref[...].astype(bf16)
+    spread = lax.dot_general(
+        jnp.concatenate([upper, lower], axis=0), jnp.concatenate([pick16, pick16], axis=0),
+        (((0,), (0,)), ((), ())), preferred_element_type=f32,
+    )
+    scale = (inverse[...] * spread).astype(bf16)
+
+    partial_copies = {}
+    for h in (1, 0):
+        turned = None
+        for b in range(blocks):
+            part = scale[b * rows : (b + 1) * rows, h * half : (h + 1) * half][None]
+            scaled = power[h, b] * part
+            power[h, b] = scaled
+            piece = lax.dot_general(
+                cleared[:, b * rows : (b + 1) * rows, :].reshape(tokens * rows, dim),
+                scaled.reshape(tokens * rows, half),
+                (((0,), (0,)), ((), ())), preferred_element_type=f32,
+            )
+            turned = piece if turned is None else turned + piece
+        span = slice(h * (groups // 2), (h + 1) * (groups // 2))
+        partial_buf[span] = jnp.transpose(turned).astype(bf16).reshape(
+            groups // 2, own_rows, dim
+        )
+        partial_copies.update(
+            exchange(
+                lambda t: partial_buf.at[t], lambda t: arrived.at[t], 3,
+                [t for t in range(groups)[span][::-1] if t],
+            )
+        )
+    crossed = jnp.sum(jnp.where(asked, mass * log_student, 0.0), axis=1, keepdims=True)
+    divergence = query_entropy[:, :1] - crossed
+    loss_buf[mine] = jnp.broadcast_to(
+        jnp.sum(weights * divergence, axis=0, keepdims=True) / weight_sum, loss_buf.shape[1:]
+    )
+    loss_copies = across(loss_buf, 1)
+
+    for b in range(blocks):
+        at = slice(b * rows, (b + 1) * rows)
+        token_grad = None
+        for h in range(2):
+            span = slice(h * (groups // 2), (h + 1) * (groups // 2))
+            piece = jnp.dot(
+                power[h, b].reshape(tokens * rows, half),
+                query_buf[span].reshape(half, dim), preferred_element_type=f32,
+            )
+            token_grad = piece if token_grad is None else token_grad + piece
+        token_grad = token_grad.reshape(tokens, rows, dim)
+        for first in range(0, tokens, bite):
+            for j in range(first, first + bite):
+                usable = jnp.full((), j, bf16) < wide16[at]
+                out_ref[j, at, :] = jnp.where(
+                    usable, token_grad[j].astype(bf16), jnp.zeros((rows, dim), bf16)
+                )
+
+    for t in partial_copies:
+        partial_copies[t].wait()
+    for copy in loss_copies:
+        copy.wait()
+    grad_ref[...] = partial_buf[0].astype(f32) + jnp.sum(
+        arrived[1:].astype(f32), axis=0
+    )
+    loss_ref[...] = jnp.sum(loss_buf[...], axis=0)[:1, :1]
+
+
+def finish_kernel(out_ref, grad_ref, loss_ref, out_hbm, grad_hbm, loss_hbm, sem):
+    copies = []
+    tokens = out_ref.shape[0]
+    pieces = sem.shape[0] - 2
+    for k in range(pieces):
+        at = pl.ds(k * (tokens // pieces), tokens // pieces)
+        copies.append(pltpu.make_async_copy(out_ref.at[at], out_hbm.at[at], sem.at[k]))
+    copies.append(pltpu.make_async_copy(grad_ref, grad_hbm, sem.at[pieces]))
+    copies.append(pltpu.make_async_copy(loss_ref, loss_hbm, sem.at[pieces + 1]))
+    for copy in copies:
+        copy.start()
+    for copy in copies:
+        copy.wait()
+
+
+def fused(queries, passages, lengths, cand_ids, owner_map, teacher, weights):
+    groups = lax.axis_size("grp")
+    replicas = lax.axis_size("rep")
+    count, _, query_len, dim = queries.shape
+    block, _, tokens, _ = passages.shape
+    ways = cand_ids.shape[2]
+    own_rows = count * query_len
+    width = groups * own_rows
+    total = groups * count
+    rows = 16
+    f32, bf16, i32 = jnp.float32, jnp.bfloat16, jnp.int32
+    dma = pltpu.SemaphoreType.DMA
+    meta_rows = -(-4 * count // 8) * 8
+    vmem = pltpu.VMEM
+    anywhere = pl.BlockSpec(memory_space=pl.ANY)
+    pieces = span_of(tokens, 5)
+    results = pl.pallas_call(
+        functools.partial(fused_kernel, groups, replicas),
+        name="fused",
+        out_shape=[
+            vmem((tokens, block, dim), bf16),
+            vmem((own_rows, dim), f32),
+            vmem((1, 1), f32),
+        ],
+        in_specs=[anywhere] * 7,
+        out_specs=[VMEM_SPEC] * 3,
+        scratch_shapes=[
+            vmem((tokens, block, dim), bf16),
+            vmem((tokens, block, 2 * dim), bf16),
+            vmem((tokens, block, dim), bf16),
+            vmem((2, tokens, rows, width // 2), f32),
+            vmem((2, block // rows, tokens, rows, width // 2), bf16),
+            vmem((block, width), f32),
+            vmem((block, width), f32),
+            vmem((groups, own_rows, dim), bf16),
+            vmem((2, width // 2, 2 * dim), bf16),
+            vmem((groups, meta_rows, LANES), f32),
+            vmem((total, groups * block), f32),
+            vmem((total, groups * block), f32),
+            vmem((total, width), f32),
+            vmem((groups, total // 2, LANES), f32),
+            vmem((replicas, 8, LANES), f32),
+            vmem((total, groups * block), f32),
+            vmem((total, LANES), f32),
+            vmem((total, LANES), f32),
+            vmem((groups, own_rows, dim), bf16),
+            vmem((groups, own_rows, dim), bf16),
+            vmem((replicas, 8, LANES), f32),
+            vmem((count, ways), i32),
+            vmem((1, groups * block), i32),
+            vmem((count, ways), f32),
+            vmem((1, count), f32),
+            vmem((1, block), i32),
+            dma((pieces,)),
+            dma((6,)),
+            dma((4, groups)),
+            dma((4, groups)),
+            dma((2, replicas)),
+            dma((2, replicas)),
+        ],
+        compiler_params=pltpu.CompilerParams(
+            collective_id=3, has_side_effects=True, vmem_limit_bytes=FUSED_VMEM
+        ),
+    )(
+        queries.reshape(own_rows, dim),
+        cand_ids[:, 0],
+        owner_map,
+        teacher[:, 0],
+        jnp.transpose(weights),
+        lengths.reshape(1, block),
+        jnp.transpose(passages[:, 0], (1, 0, 2)),
+    )
+    passage_grad, query_grad, loss = pl.pallas_call(
+        finish_kernel,
+        name="finish",
+        out_shape=[
+            jax.ShapeDtypeStruct((tokens, block, dim), bf16),
+            jax.ShapeDtypeStruct((own_rows, dim), f32),
+            jax.ShapeDtypeStruct((1, 1), f32),
+        ],
+        in_specs=[VMEM_SPEC] * 3,
+        out_specs=[anywhere] * 3,
+        scratch_shapes=[dma((pieces + 2,))],
+    )(*(pltpu.with_memory_space_constraint(x, pltpu.VMEM) for x in results))
+    return (
+        loss.reshape(()),
+        query_grad.reshape(count, 1, query_len, dim),
+        jnp.transpose(passage_grad, (1, 0, 2))[:, None],
+    )
+
+
+FUSED_VMEM = 52 * 2**20
+
+
+def fits(groups, queries, passages):
+    width = groups * queries.shape[0] * queries.shape[2]
+    block, _, tokens, dim = passages.shape
+    need = tokens * width * (2 * block + 4 * 16) + 10 * tokens * block * dim
+    need += 8 * width * (2 * block + 2 * dim)
+    whole = groups & (groups - 1) == 0 and groups > 1 and width % (2 * LANES) == 0
+    return whole and 2 * block == LANES and dim == LANES and tokens <= 256 and need < FUSED_VMEM
+
+
+def step(*args):
+    if fits(lax.axis_size("grp"), args[0], args[1]):
+        return fused(*args)
+    return on_device(*args)
+
+
 def solution(mesh):
     return jax.shard_map(
-        on_device,
+        step,
         mesh=mesh,
         in_specs=(
             P("grp", "rep", None, None),

time: 60.5 us -> 31.8 us (0.53)
  Pallas kernels: 56.3 us -> 30.9 us
  between operations: 2.47 us -> 0.64 us
  local copies, waits for them, and re-layouts: 1.38 us -> 0 us
    pallas_call x5 -> x2, Pallas kernels: 56.3 us -> 30.9 us  [the longest x1 28.7 us: fused(): pl.pallas_call(functools.partial(fused_kernel, groups, replicas), name='f...]
    unnamed x1 -> x0, local copies, waits for them, and re-layouts: 1.38 us -> none
where the time goes in v1:
time: 31.8 us; the launch traced here: 31.6 us
  Pallas kernels  30.9 us (97%)
  between operations  0.64 us (2%)
    pallas_call x1, Pallas kernels, fused(): pl.pallas_call(functools.partial(fused_kernel, groups, replicas), name='f...  28.7 us
    pallas_call x1, Pallas kernels, fused(): pl.pallas_call(finish_kernel, name='finish', out_shape=[jax.ShapeDtypeStr...  2.29 us

profile of v1, /device:TPU:0, one launch (start us, length us, event | category | flops | bytes accessed | tf_op | source)
XLA Modules:
  0.0 31.6 jit_solution(4155753341157340548)
XLA Ops:
  0.6 28.7 %fused.1 = (bf16[180,64,128]{2,1,0:T(8,128)(2,1)S(1)}, f32[64,128]{1,0:T(8,128)S(1)}, f32[1,1]{1,0:T(1,128)}) custom-call(bf16[64,128]{1,0:T(8,128)(2,1)} %bitcast.16, s32[2,64]{1,0:T(2,128)} %bitcast.17, s32[1,512]{1,0:T(1,128)} %map_hbm.1, f32[2,64]{1,0:T(2,128)} %bitcast.18, f32[1,2]{1,0:T(1,128)} %bitcast.19, s32[1,64]{1,0:T(1,128)} %bitcast.20, ...), custom_call_target="tpu_custom_call" | custom-call | tf_op jit(solution)/shard_map/fused/pallas_call | solution.py:847
  29.3 2.3 %finish.1 = (bf16[180,64,128]{2,1,0:T(8,128)(2,1)}, f32[64,128]{1,0:T(8,128)}, f32[1,1]{1,0:T(1,128)}) custom-call(bf16[180,64,128]{2,1,0:T(8,128)(2,1)S(1)} %get-tuple-element.9.out_ref, f32[64,128]{1,0:T(8,128)S(1)} %get-tuple-element.10.grad_ref, f32[1,1]{1,0:T(1,128)} %get-tuple-element.11.loss_ref), custom_call_target="tpu_custom_call" | custom-call | tf_op jit(solution)/shard_map/finish/pallas_call | solution.py:903

commit v2 on v1

--- a/solution.py
+++ b/solution.py
@@ -544,8 +544,8 @@
 def fused_kernel(
     groups, replicas,
     queries_hbm, cand_hbm, map_hbm, teacher_hbm, weights_hbm, lengths_hbm, passages_hbm,
-    out_ref, grad_ref, loss_ref,
-    raw, doubled, cleared, held, power, inverse, lse, query_buf, folded, meta_buf,
+    out_ref, grad_ref,
+    raw, doubled, cleared, turned_ref, tops, scales, limits, held, power, inverse, lse, query_buf, folded, meta_buf,
     hits_ref, mass_ref, pick_ref, score_buf, weight_buf, grade_buf, query_weight, query_entropy,
     partial_buf, arrived, loss_buf, cand_ref, map_ref, teacher_ref, weights_ref, lengths_ref,
     load_sem, small_sem, send_sem, recv_sem, wsend_sem, wrecv_sem,
@@ -647,54 +647,76 @@
             here = raw[at]
             usable = at.astype(f32).astype(bf16) < wide16
             known = jnp.where(usable, here, first_token)
-            doubled[at, :, :dim] = known
-            doubled[at, :, dim:] = known
-            cleared[at] = jnp.where(usable, here, jnp.zeros_like(here))
+            doubled[:, at] = known.reshape(blocks, rows, dim)
+            cleared[:, at] = jnp.where(usable, here, jnp.zeros_like(here)).reshape(
+                blocks, rows, dim
+            )
         return 0
 
     lax.fori_loop(0, tokens // prep, prepare, 0)
 
-    bite = span_of(tokens, 4)
+    single = jnp.minimum(me + 1, 1)
+    bite = span_of(tokens, 180)
     units = [(h, b) for h in range(2) for b in range(blocks)]
-    above = None
-    for u in range(len(units) + 1):
-        if u < len(units):
-            h, b = units[u]
-            if b == 0:
-                span = slice(h * (groups // 2), (h + 1) * (groups // 2))
-                for t in range(groups)[span]:
-                    if t:
-                        query_copies[t].wait()
-                scaled = query_buf[span].reshape(half, dim).astype(f32) * to_base2
-                upper = scaled.astype(bf16)
-                folded[h, :, :dim] = upper
-                folded[h, :, dim:] = (scaled - upper.astype(f32)).astype(bf16)
+
+    def forward(u):
+        ahead = units[u] if u < len(units) else None
+        behind = units[u - 1] if u > 0 else None
+        highest = None
+        if ahead is not None:
+            h, b = ahead
+            left = doubled[b].reshape(tokens * rows, dim)
             products = lax.dot_general(
-                doubled[:, b * rows : (b + 1) * rows, :].reshape(tokens * rows, 2 * dim),
-                folded[h], (((1,), (1,)), ((), ())), preferred_element_type=f32,
+                jnp.concatenate([left, left], axis=1), folded[h],
+                (((1,), (1,)), ((), ())), preferred_element_type=f32,
             ).reshape(tokens, rows, half)
-            highest = None
-        if u > 0:
-            h0, b0 = units[u - 1]
-            summed = jnp.zeros((rows, half), f32)
-        for first in range(0, tokens, bite):
-            at = slice(first, first + bite)
-            if u < len(units):
-                held[u % 2, at] = products[at]
-                top = jnp.max(products[at], axis=0)
-                highest = top if highest is None else jnp.maximum(highest, top)
-            if u > 0:
-                powers = jnp.exp2(held[(u - 1) % 2, at] - above[None])
-                power[h0, b0, at] = powers.astype(bf16)
-                summed = summed + jnp.sum(powers, axis=0)
-        if u > 0:
+        if behind is not None:
+            h0, b0 = behind
+            above = tops[(u - 1) % 2]
+            sums = [None] * 2
+        peaks = [None] * 2
+        for first in range(tokens // 2):
+            for line in range(2):
+                j = line * (tokens // 2) + first
+                if ahead is not None:
+                    held[u % 2, j] = products[j]
+                    peaks[line] = products[j] if first == 0 else jnp.maximum(peaks[line], products[j])
+                if behind is not None:
+                    powers = jnp.exp2(held[(u - 1) % 2, j] - above)
+                    power[h0, b0, j] = powers.astype(bf16)
+                    sums[line] = powers if first == 0 else sums[line] + powers
+        if ahead is not None:
+            highest = functools.reduce(jnp.maximum, peaks)
+        if behind is not None:
+            summed = functools.reduce(jnp.add, sums)
+        if ahead is not None:
+            tops[u % 2] = highest
+        if behind is not None:
             at = slice(b0 * rows, (b0 + 1) * rows)
             to = slice(h0 * half, (h0 + 1) * half)
-            unused = (tokens - wide[at, :1]) * jnp.exp2(held[(u - 1) % 2, 0] - above)
+            unused = (tokens - limits[at, :1]) * jnp.exp2(held[(u - 1) % 2, 0] - above)
             summed = summed - unused
             lse[at, to] = above + jnp.log2(summed)
             inverse[at, to] = 1.0 / summed
-        above = highest
+
+    limits[...] = wide
+    for u in range(len(units) + 1):
+        if u < len(units) and units[u][1] == 0:
+            h = units[u][0]
+            span = slice(h * (groups // 2), (h + 1) * (groups // 2))
+            for t in range(groups)[span]:
+                if t:
+                    query_copies[t].wait()
+            scaled = query_buf[span].reshape(half, dim).astype(f32) * to_base2
+            upper = scaled.astype(bf16)
+            folded[h, :, :dim] = upper
+            folded[h, :, dim:] = (scaled - upper.astype(f32)).astype(bf16)
+
+        def trip(_, carry, u=u):
+            forward(u)
+            return carry
+
+        lax.fori_loop(0, single, trip, 0)
 
     scores = lax.dot_general(
         pick_ref[...], lse[...] * (1.0 / to_base2), (((1,), (1,)), ((), ())),
@@ -714,6 +736,8 @@
     )
     weight_copies = across(weight_buf, 0)
     place_candidates(count, ways, meta_buf, hits_ref, mass_ref)
+    for b in range(blocks):
+        turned_ref[b] = jnp.transpose(cleared[b].reshape(tokens * rows, dim))
     for copy in weight_copies:
         copy.wait()
     weights = query_weight[:, :1]
@@ -754,24 +778,29 @@
         (((0,), (0,)), ((), ())), preferred_element_type=f32,
     )
     scale = (inverse[...] * spread).astype(bf16)
+    for h in range(2):
+        for b in range(blocks):
+            scales[h, b] = scale[b * rows : (b + 1) * rows, h * half : (h + 1) * half]
 
     partial_copies = {}
     for h in (1, 0):
-        turned = None
-        for b in range(blocks):
-            part = scale[b * rows : (b + 1) * rows, h * half : (h + 1) * half][None]
-            scaled = power[h, b] * part
-            power[h, b] = scaled
-            piece = lax.dot_general(
-                cleared[:, b * rows : (b + 1) * rows, :].reshape(tokens * rows, dim),
-                scaled.reshape(tokens * rows, half),
-                (((0,), (0,)), ((), ())), preferred_element_type=f32,
-            )
-            turned = piece if turned is None else turned + piece
+
+        def backward(_, carry, h=h):
+            added = None
+            for b in range(blocks):
+                piece = jnp.dot(
+                    turned_ref[b],
+                    (power[h, b] * scales[h, b][None]).reshape(tokens * rows, half),
+                    preferred_element_type=f32,
+                )
+                added = piece if added is None else added + piece
+            partial_buf[h * (groups // 2) : (h + 1) * (groups // 2)] = (
+                jnp.transpose(added).astype(bf16).reshape(groups // 2, own_rows, dim)
+            )
+            return carry
+
+        lax.fori_loop(0, single, backward, 0)
         span = slice(h * (groups // 2), (h + 1) * (groups // 2))
-        partial_buf[span] = jnp.transpose(turned).astype(bf16).reshape(
-            groups // 2, own_rows, dim
-        )
         partial_copies.update(
             exchange(
                 lambda t: partial_buf.at[t], lambda t: arrived.at[t], 3,
@@ -785,45 +814,52 @@
     )
     loss_copies = across(loss_buf, 1)
 
-    for b in range(blocks):
-        at = slice(b * rows, (b + 1) * rows)
-        token_grad = None
-        for h in range(2):
-            span = slice(h * (groups // 2), (h + 1) * (groups // 2))
-            piece = jnp.dot(
-                power[h, b].reshape(tokens * rows, half),
-                query_buf[span].reshape(half, dim), preferred_element_type=f32,
-            )
-            token_grad = piece if token_grad is None else token_grad + piece
-        token_grad = token_grad.reshape(tokens, rows, dim)
-        for first in range(0, tokens, bite):
-            for j in range(first, first + bite):
-                usable = jnp.full((), j, bf16) < wide16[at]
+    def tokenwise(_, carry):
+        for b in range(blocks):
+            at = slice(b * rows, (b + 1) * rows)
+            token_grad = None
+            for h in range(2):
+                span = slice(h * (groups // 2), (h + 1) * (groups // 2))
+                piece = jnp.dot(
+                    (power[h, b] * scales[h, b][None]).reshape(tokens * rows, half),
+                    query_buf[span].reshape(half, dim), preferred_element_type=f32,
+                )
+                token_grad = piece if token_grad is None else token_grad + piece
+            token_grad = token_grad.reshape(tokens, rows, dim)
+            limit = limits[at].astype(bf16)
+            for j in range(tokens):
+                usable = jnp.full((), j, bf16) < limit
                 out_ref[j, at, :] = jnp.where(
                     usable, token_grad[j].astype(bf16), jnp.zeros((rows, dim), bf16)
                 )
+        return carry
+
+    lax.fori_loop(0, single, tokenwise, 0)
 
     for t in partial_copies:
         partial_copies[t].wait()
     for copy in loss_copies:
         copy.wait()
-    grad_ref[...] = partial_buf[0].astype(f32) + jnp.sum(
+    grad_ref[:own_rows, :] = partial_buf[0].astype(f32) + jnp.sum(
         arrived[1:].astype(f32), axis=0
     )
-    loss_ref[...] = jnp.sum(loss_buf[...], axis=0)[:1, :1]
-
-
-def finish_kernel(out_ref, grad_ref, loss_ref, out_hbm, grad_hbm, loss_hbm, sem):
+    grad_ref[own_rows:, :] = jnp.sum(loss_buf[...], axis=0)
+
+
+def finish_kernel(out_ref, grad_ref, out_hbm, grad_hbm, loss_hbm, loss_ref, sem):
     copies = []
     tokens = out_ref.shape[0]
     pieces = sem.shape[0] - 2
     for k in range(pieces):
         at = pl.ds(k * (tokens // pieces), tokens // pieces)
         copies.append(pltpu.make_async_copy(out_ref.at[at], out_hbm.at[at], sem.at[k]))
-    copies.append(pltpu.make_async_copy(grad_ref, grad_hbm, sem.at[pieces]))
+        copies[-1].start()
+    own = grad_hbm.shape[0]
+    copies.append(pltpu.make_async_copy(grad_ref.at[pl.ds(0, own)], grad_hbm, sem.at[pieces]))
+    copies[-1].start()
+    loss_ref[...] = grad_ref[own : own + 1, :1]
     copies.append(pltpu.make_async_copy(loss_ref, loss_hbm, sem.at[pieces + 1]))
-    for copy in copies:
-        copy.start()
+    copies[-1].start()
     for copy in copies:
         copy.wait()
 
@@ -849,15 +885,18 @@
         name="fused",
         out_shape=[
             vmem((tokens, block, dim), bf16),
-            vmem((own_rows, dim), f32),
-            vmem((1, 1), f32),
+            vmem((own_rows + 8, dim), f32),
         ],
         in_specs=[anywhere] * 7,
-        out_specs=[VMEM_SPEC] * 3,
+        out_specs=[VMEM_SPEC] * 2,
         scratch_shapes=[
             vmem((tokens, block, dim), bf16),
-            vmem((tokens, block, 2 * dim), bf16),
-            vmem((tokens, block, dim), bf16),
+            vmem((block // rows, tokens, rows, dim), bf16),
+            vmem((block // rows, tokens, rows, dim), bf16),
+            vmem((block // rows, dim, tokens * rows), bf16),
+            vmem((2, rows, width // 2), f32),
+            vmem((2, block // rows, rows, width // 2), bf16),
+            vmem((block, LANES), f32),
             vmem((2, tokens, rows, width // 2), f32),
             vmem((2, block // rows, tokens, rows, width // 2), bf16),
             vmem((block, width), f32),
@@ -908,9 +947,9 @@
             jax.ShapeDtypeStruct((own_rows, dim), f32),
             jax.ShapeDtypeStruct((1, 1), f32),
         ],
-        in_specs=[VMEM_SPEC] * 3,
+        in_specs=[VMEM_SPEC] * 2,
         out_specs=[anywhere] * 3,
-        scratch_shapes=[dma((pieces + 2,))],
+        scratch_shapes=[vmem((1, 1), f32), dma((pieces + 2,))],
     )(*(pltpu.with_memory_space_constraint(x, pltpu.VMEM) for x in results))
     return (
         loss.reshape(()),

time: 31.8 us -> 30.1 us (0.947)
  Pallas kernels: 30.9 us -> 29 us
    pallas_call x1, Pallas kernels: 28.7 us -> 27.4 us  [fused(): pl.pallas_call(functools.partial(fused_kernel, groups, replicas), name='f...]
    pallas_call x1, Pallas kernels: 2.29 us -> 1.66 us  [fused(): pl.pallas_call(finish_kernel, name='finish', out_shape=[jax.ShapeDtypeStr...]
where the time goes in v2:
time: 30.1 us; the launch traced here: 29.8 us
  Pallas kernels  29 us (96%)
  between operations  0.8 us (3%)
    pallas_call x1, Pallas kernels, fused(): pl.pallas_call(functools.partial(fused_kernel, groups, replicas), name='f...  27.4 us
    pallas_call x1, Pallas kernels, fused(): pl.pallas_call(finish_kernel, name='finish', out_shape=[jax.ShapeDtypeStr...  1.66 us

profile of v2, /device:TPU:0, one launch (start us, length us, event | category | flops | bytes accessed | tf_op | source)
XLA Modules:
  0.0 29.8 jit_solution(17281418589684638355)
XLA Ops:
  0.6 27.4 %fused.1 = (bf16[180,64,128]{2,1,0:T(8,128)(2,1)S(1)}, f32[72,128]{1,0:T(8,128)S(1)}) custom-call(bf16[64,128]{1,0:T(8,128)(2,1)} %bitcast.16, s32[2,64]{1,0:T(2,128)} %bitcast.17, s32[1,512]{1,0:T(1,128)} %map_hbm.1, f32[2,64]{1,0:T(2,128)} %bitcast.18, f32[1,2]{1,0:T(1,128)} %bitcast.19, s32[1,64]{1,0:T(1,128)} %bitcast.20, bf16[180,64,128]{2,1,0:T(8,128)(2,1)} %bitcast.15), custom_call_target="tpu_custom_call" | custom-call | tf_op jit(solution)/shard_map/fused/pallas_call | solution.py:883
  28.0 1.7 %finish.1 = (bf16[180,64,128]{2,1,0:T(8,128)(2,1)}, f32[64,128]{1,0:T(8,128)}, f32[1,1]{1,0:T(1,128)}) custom-call(bf16[180,64,128]{2,1,0:T(8,128)(2,1)S(1)} %get-tuple-element.8.out_ref, f32[72,128]{1,0:T(8,128)S(1)} %get-tuple-element.9.grad_ref), custom_call_target="tpu_custom_call" | custom-call | tf_op jit(solution)/shard_map/finish/pallas_call | solution.py:942
